TPU v7x, 32 devices: a 4x4x1 block of a 4x4x8 slice. The times are simulated.
32 devices in a mesh: b: 1 (over z), rep: 4 (over y), col: 4 (over x), row: 2 (over core).
Axes of the slice: x: 4, y: 4, z: 1, core: 2. Of those that a mesh axis runs over, the one named last changes fastest.
The devices are a block of a 4x4x8 slice.
Arguments:
- a_blocks: float32 [36, 36, 128, 128], P(('b', 'row'), 'col')
Outputs:
- output: float32 [36, 36, 128, 128], P(('b', 'row'), 'col')
All inputs are finite; a program needn't handle non-finite values.
Results may differ from a plain program's by a relative error of at most 0.001.
Values sent between devices are 32-bit elements.
A program may use at most 768 MiB of HBM per device.

v0:
```python
import jax
import jax.numpy as jnp
from jax import lax
from jax.sharding import PartitionSpec as P


def solution(mesh):
    row_size = mesh.shape["row"]
    col_size = mesh.shape["col"]
    rep_size = mesh.shape["rep"]
    grid_spec = P(("b", "row"), "col")

    def local_factor(a_loc):
        rows_blk, cols_blk, blk_size, _ = a_loc.shape
        num_steps = rows_blk * row_size
        share_len = blk_size // rep_size
        row_idx = lax.axis_index("row")
        col_idx = lax.axis_index("col")
        rep_idx = lax.axis_index("rep")
        work_mat = jnp.where(rep_idx == 0, a_loc, 0.0)
        out_cols = [jnp.zeros((rows_blk, blk_size, blk_size), jnp.float32)] * cols_blk
        for step_idx in range(num_steps):
            step_row = step_idx % row_size
            step_col = step_idx % col_size
            first_row = step_idx // row_size
            first_col = step_idx // col_size
            tail_rows = rows_blk - first_row
            col_sum = lax.psum(work_mat[first_row:, first_col], "rep")
            diag_mine = jnp.where(row_idx == step_row, col_sum[0], 0.0)
            diag_fac = jnp.tril(jnp.linalg.cholesky(lax.psum(diag_mine, "row")))
            solved = lax.linalg.triangular_solve(
                diag_fac, col_sum.reshape(tail_rows * blk_size, blk_size),
                left_side=False, lower=True, transpose_a=True,
            ).reshape(tail_rows, blk_size, blk_size)
            glob_row = ((first_row + jnp.arange(tail_rows)) * row_size + row_idx)[:, None, None]
            panel_blk = jnp.where(glob_row > step_idx, solved, jnp.where(glob_row == step_idx, diag_fac, 0.0))
            is_owner = col_idx == step_col
            padded = jnp.pad(panel_blk, ((first_row, 0), (0, 0), (0, 0)))
            out_cols[first_col] = jnp.where(is_owner, padded, out_cols[first_col])
            if step_idx < num_steps - 1:
                panel_row = lax.psum(jnp.where(is_owner, panel_blk, 0.0), "col")
                gathered = lax.all_gather(panel_row, "row", axis=1)
                col_full = jnp.pad(
                    gathered.reshape(tail_rows * row_size, blk_size, blk_size),
                    ((first_row * row_size, 0), (0, 0), (0, 0)),
                )
                col_grid = col_full.reshape(cols_blk, col_size, blk_size, blk_size)[first_col:]
                panel_col = lax.dynamic_index_in_dim(col_grid, col_idx, axis=1, keepdims=False)
                row_share = lax.dynamic_slice_in_dim(panel_row, rep_idx * share_len, share_len, axis=2)
                col_share = lax.dynamic_slice_in_dim(panel_col, rep_idx * share_len, share_len, axis=2)
                update = jnp.einsum(
                    "tak,uck->tuac", row_share, col_share,
                    precision=lax.Precision.HIGHEST, preferred_element_type=jnp.float32,
                )
                trail_new = work_mat[first_row:, first_col:] - update
                work_mat = lax.dynamic_update_slice(work_mat, trail_new, (first_row, first_col, 0, 0))
        return jnp.stack(out_cols, axis=1)

    return jax.shard_map(local_factor, mesh=mesh, in_specs=grid_spec, out_specs=grid_spec, check_vma=False)
```

profile of v0, /device:TPU:103, one launch (start us, length us, event | category | flops | bytes accessed | tf_op | source)
XLA Modules:
  0.0 5253.6 jit_solution(14863281403876225631)
XLA Ops:
  17.1 42.4 all-reduce.159.cloned.1.call-done
  112.4 40.7 all-reduce.163.cloned.1.call-done
  186.5 40.6 all-reduce.165.cloned.1.call-done
  279.8 40.7 all-reduce.169.cloned.1.call-done
  354.0 40.1 all-reduce.171.cloned.1.call-done
  447.2 40.2 all-reduce.175.cloned.1.call-done
  522.0 40.1 all-reduce.177.cloned.1.call-done
  615.1 40.2 all-reduce.181.cloned.1.call-done
  689.8 39.6 all-reduce.183.cloned.1.call-done
  782.4 39.5 all-reduce.187.cloned.1.call-done
  852.5 39.7 all-reduce.189.cloned.1.call-done
  945.2 39.5 all-reduce.193.cloned.1.call-done
  1015.2 39.1 all-reduce.195.cloned.1.call-done
  1107.0 38.7 all-reduce.199.cloned.1.call-done
  1176.9 39.1 all-reduce.201.cloned.1.call-done
  1268.7 38.7 all-reduce.205.cloned.1.call-done
  1338.7 38.8 all-reduce.207.cloned.1.call-done
  1430.1 38.1 all-reduce.211.cloned.1.call-done
  1496.0 38.7 all-reduce.213.cloned.1.call-done
  1587.4 38.1 all-reduce.217.cloned.1.call-done
  1653.4 38.6 all-reduce.219.cloned.1.call-done
  1744.4 37.6 all-reduce.223.cloned.1.call-done
  1810.8 38.6 all-reduce.225.cloned.1.call-done
  1901.6 37.6 all-reduce.229.cloned.1.call-done
  1967.8 38.1 all-reduce.231.cloned.1.call-done
  2057.9 37.0 all-reduce.235.cloned.1.call-done
  2121.0 38.1 all-reduce.237.cloned.1.call-done
  2211.1 37.0 all-reduce.241.cloned.1.call-done
  2274.2 37.7 all-reduce.243.cloned.1.call-done
  2426.2 37.7 all-reduce.249.cloned.1.call-done
  2578.2 37.3 all-reduce.255.cloned.1.call-done
  2724.6 37.3 all-reduce.261.cloned.1.call-done
  (1098 shorter events, 3989.8 us)
Async XLA Ops:
  61.1 92.0 %all-reduce.163.cloned.1.call-start = ((), (), s32[]{:S(2)}) async-start(), calls=%async_computation.2 | async-start | bytes 2359296 | tf_op jit(solution)/shard_map/psum | solution.py:41
  228.6 91.8 %all-reduce.169.cloned.1.call-start = ((), (), s32[]{:S(2)}) async-start(), calls=%async_computation.5 | async-start | bytes 2359296 | tf_op jit(solution)/shard_map/psum | solution.py:41
  395.6 91.9 %all-reduce.175.cloned.1.call-start = ((), (), s32[]{:S(2)}) async-start(), calls=%async_computation.8 | async-start | bytes 2228224 | tf_op jit(solution)/shard_map/psum | solution.py:41
  563.6 91.7 %all-reduce.181.cloned.1.call-start = ((), (), s32[]{:S(2)}) async-start(), calls=%async_computation.11 | async-start | bytes 2228224 | tf_op jit(solution)/shard_map/psum | solution.py:41
  731.0 90.9 %all-reduce.187.cloned.1.call-start = ((), (), s32[]{:S(2)}) async-start(), calls=%async_computation.14 | async-start | bytes 2097152 | tf_op jit(solution)/shard_map/psum | solution.py:41
  893.7 91.0 %all-reduce.193.cloned.1.call-start = ((), (), s32[]{:S(2)}) async-start(), calls=%async_computation.17 | async-start | bytes 2097152 | tf_op jit(solution)/shard_map/psum | solution.py:41
  1055.9 89.9 %all-reduce.199.cloned.1.call-start = ((), (), s32[]{:S(2)}) async-start(), calls=%async_computation.20 | async-start | bytes 1966080 | tf_op jit(solution)/shard_map/psum | solution.py:41
  1217.6 89.9 %all-reduce.205.cloned.1.call-start = ((), (), s32[]{:S(2)}) async-start(), calls=%async_computation.23 | async-start | bytes 1966080 | tf_op jit(solution)/shard_map/psum | solution.py:41
  1379.0 89.2 %all-reduce.211.cloned.1.call-start = ((), (), s32[]{:S(2)}) async-start(), calls=%async_computation.26 | async-start | bytes 1835008 | tf_op jit(solution)/shard_map/psum | solution.py:41
  1536.2 89.2 %all-reduce.217.cloned.1.call-start = ((), (), s32[]{:S(2)}) async-start(), calls=%async_computation.29 | async-start | bytes 1835008 | tf_op jit(solution)/shard_map/psum | solution.py:41
  1693.5 88.5 %all-reduce.223.cloned.1.call-start = ((), (), s32[]{:S(2)}) async-start(), calls=%async_computation.32 | async-start | bytes 1703936 | tf_op jit(solution)/shard_map/psum | solution.py:41
  1850.9 88.3 %all-reduce.229.cloned.1.call-start = ((), (), s32[]{:S(2)}) async-start(), calls=%async_computation.35 | async-start | bytes 1703936 | tf_op jit(solution)/shard_map/psum | solution.py:41
  2007.4 87.5 %all-reduce.235.cloned.1.call-start = ((), (), s32[]{:S(2)}) async-start(), calls=%async_computation.38 | async-start | bytes 1572864 | tf_op jit(solution)/shard_map/psum | solution.py:41
  2160.7 87.5 %all-reduce.241.cloned.1.call-start = ((), (), s32[]{:S(2)}) async-start(), calls=%async_computation.41 | async-start | bytes 1572864 | tf_op jit(solution)/shard_map/psum | solution.py:41
  2313.4 86.8 %all-reduce.247.cloned.1.call-start = ((), (), s32[]{:S(2)}) async-start(), calls=%async_computation.44 | async-start | bytes 1441792 | tf_op jit(solution)/shard_map/psum | solution.py:41
  2465.4 87.0 %all-reduce.253.cloned.1.call-start = ((), (), s32[]{:S(2)}) async-start(), calls=%async_computation.47 | async-start | bytes 1441792 | tf_op jit(solution)/shard_map/psum | solution.py:41
  2616.9 86.2 %all-reduce.259.cloned.1.call-start = ((), (), s32[]{:S(2)}) async-start(), calls=%async_computation.50 | async-start | bytes 1310720 | tf_op jit(solution)/shard_map/psum | solution.py:41
  2763.4 90.1 %all-reduce.265.cloned.1.call-start = ((), (), s32[]{:S(2)}) async-start(), calls=%async_computation.53 | async-start | bytes 1310720 | tf_op jit(solution)/shard_map/psum | solution.py:41
  2914.0 85.7 %all-reduce.271.cloned.1.call-start = ((), (), s32[]{:S(2)}) async-start(), calls=%async_computation.56 | async-start | bytes 1179648 | tf_op jit(solution)/shard_map/psum | solution.py:41
  3059.9 89.1 %all-reduce.277.cloned.1.call-start = ((), (), s32[]{:S(2)}) async-start(), calls=%async_computation.59 | async-start | bytes 1179648 | tf_op jit(solution)/shard_map/psum | solution.py:41
  3208.9 85.2 %all-reduce.283.cloned.1.call-start = ((), (), s32[]{:S(2)}) async-start(), calls=%async_computation.62 | async-start | bytes 1048576 | tf_op jit(solution)/shard_map/psum | solution.py:41
  3351.6 85.3 %all-reduce.289.cloned.1.call-start = ((), (), s32[]{:S(2)}) async-start(), calls=%async_computation.65 | async-start | bytes 1048576 | tf_op jit(solution)/shard_map/psum | solution.py:41
  3494.5 84.9 %all-reduce.295.cloned.1.call-start = ((), (), s32[]{:S(2)}) async-start(), calls=%async_computation.68 | async-start | bytes 917504 | tf_op jit(solution)/shard_map/psum | solution.py:41
  3626.9 84.8 %all-reduce.301.cloned.1.call-start = ((), (), s32[]{:S(2)}) async-start(), calls=%async_computation.71 | async-start | bytes 917504 | tf_op jit(solution)/shard_map/psum | solution.py:41
  3758.5 84.4 %all-reduce.307.cloned.1.call-start = ((), (), s32[]{:S(2)}) async-start(), calls=%async_computation.74 | async-start | bytes 786432 | tf_op jit(solution)/shard_map/psum | solution.py:41
  3888.7 84.3 %all-reduce.313.cloned.1.call-start = ((), (), s32[]{:S(2)}) async-start(), calls=%async_computation.77 | async-start | bytes 786432 | tf_op jit(solution)/shard_map/psum | solution.py:41
  4018.5 84.1 %all-reduce.319.cloned.1.call-start = ((), (), s32[]{:S(2)}) async-start(), calls=%async_computation.80 | async-start | bytes 655360 | tf_op jit(solution)/shard_map/psum | solution.py:41
  4147.1 84.0 %all-reduce.325.cloned.1.call-start = ((), (), s32[]{:S(2)}) async-start(), calls=%async_computation.83 | async-start | bytes 655360 | tf_op jit(solution)/shard_map/psum | solution.py:41
  4275.3 83.7 %all-reduce.331.cloned.1.call-start = ((), (), s32[]{:S(2)}) async-start(), calls=%async_computation.86 | async-start | bytes 524288 | tf_op jit(solution)/shard_map/psum | solution.py:41
  4786.9 93.3 %all-reduce.355.cloned.1.call-start = ((), (), s32[]{:S(2)}) async-start(), calls=%async_computation.98 | async-start | bytes 262144 | tf_op jit(solution)/shard_map/psum | solution.py:41
  4923.7 93.2 %all-reduce.361.cloned.1.call-start = ((), (), s32[]{:S(2)}) async-start(), calls=%async_computation.101 | async-start | bytes 262144 | tf_op jit(solution)/shard_map/psum | solution.py:41
  5060.7 84.5 %all-reduce.367.cloned.1.call-start = ((), (), s32[]{:S(2)}) async-start(), calls=%async_computation.104 | async-start | bytes 131072 | tf_op jit(solution)/shard_map/psum | solution.py:41
  (182 other events, 9094.4 us)
Sparse Core Ops, SparseCore 0:
  17.1 42.3 all-reduce.158
  112.4 40.5 all-reduce.162
  186.5 40.4 all-reduce.164
  279.8 40.5 all-reduce.168
  354.0 39.9 all-reduce.170
  447.3 40.1 all-reduce.174
  522.0 40.0 all-reduce.176
  615.2 40.1 all-reduce.180
  689.9 39.5 all-reduce.182
  782.5 39.4 all-reduce.186
  852.6 39.5 all-reduce.188
  945.2 39.4 all-reduce.192
  1015.3 39.0 all-reduce.194
  1107.1 38.6 all-reduce.198
  1177.0 39.0 all-reduce.200
  1268.8 38.6 all-reduce.204
  1338.7 38.6 all-reduce.206
  1430.1 37.9 all-reduce.210
  1496.0 38.6 all-reduce.212
  1587.5 37.9 all-reduce.216
  1653.5 38.4 all-reduce.218
  1744.4 37.5 all-reduce.222
  1810.8 38.4 all-reduce.224
  1901.6 37.4 all-reduce.228
  1967.8 38.0 all-reduce.230
  2057.9 36.9 all-reduce.234
  2121.1 38.0 all-reduce.236
  2211.2 36.9 all-reduce.240
  2274.3 37.6 all-reduce.242
  2426.3 37.5 all-reduce.248
  2578.2 37.1 all-reduce.254
  2724.6 37.1 all-reduce.260
  (97 shorter events, 2454.5 us)
where the time goes:
time: 5270 us; the launch traced here: 5250 us
  waiting for transfers between devices  3730 us (71%)
  other arithmetic  989 us (19%)
  matrix products  255 us (5%)
  local copies, waits for them, and re-layouts  171 us (3%)
  blocking collectives  58.7 us (1%)
    psum x36, waiting for transfers between devices, local_factor(): col_sum = lax.psum(work_mat[first_row:, first_col], 'rep')  1340 us
    psum x35, waiting for transfers between devices, local_factor(): panel_row = lax.psum(jnp.where(is_owner, panel_blk, 0.0), 'col')  1280 us
    psum x36, waiting for transfers between devices, local_factor(): diag_fac = jnp.tril(jnp.linalg.cholesky(lax.psum(diag_mine, 'row')))  775 us
    another operation x108, other arithmetic, local_factor(): diag_fac = jnp.tril(jnp.linalg.cholesky(lax.psum(diag_mine, 'row')))  450 us
    another operation x72, other arithmetic, local_factor(): lax.linalg.triangular_solve(diag_fac, col_sum.reshape(tail_rows * blk_siz...  380 us
    all_gather x22, waiting for transfers between devices, local_factor(): gathered = lax.all_gather(panel_row, 'row', axis=1)  328 us
    dot_general x35, matrix products, local_factor(): jnp.einsum('tak,uck->tuac', row_share, col_share, precision=lax.Precision...  188 us
  transfers between devices with their start and end apart: 129, of which 129 were waited for; matrix products, arithmetic and copies ran while one was open for 0% of the time, Pallas kernels for 0%

commit v1 on v0

v1 whole, which is shorter than its diff:
```python
import functools

import jax
import jax.numpy as jnp
from jax import lax
from jax.experimental import pallas as pl
from jax.experimental.pallas import tpu as pltpu
from jax.sharding import PartitionSpec as P

SUB = 8
MESH = pl.DeviceIdType.MESH


def dot_nt(lhs, rhs):
    return lax.dot_general(
        lhs, rhs, (((1,), (1,)), ((), ())),
        precision=lax.Precision.HIGHEST, preferred_element_type=jnp.float32,
    )


def lane_bcast(vec, lane):
    return jnp.broadcast_to(vec[:, lane:lane + 1], vec.shape)


def sub_bcast(vec, row):
    return jnp.broadcast_to(vec[row:row + 1, :], vec.shape)


def tree_sum(terms):
    while len(terms) > 1:
        terms = [sum(terms[a:a + 2][1:], terms[a]) for a in range(0, len(terms), 2)]
    return terms[0]


def factor_block(mat, put_u, put_w):
    panels = len(mat)
    shape = mat[0].shape
    lane = lax.broadcasted_iota(jnp.int32, shape, 1)
    sub = lax.broadcasted_iota(jnp.int32, shape, 0)
    aug = [jnp.where(lane == sub + SUB * q, 1.0, 0.0).astype(jnp.float32) for q in range(panels)]
    for p in range(panels):
        base = SUB * p
        cols = [lane_bcast(mat[p], base + j) for j in range(SUB)]
        piv = {(i, j): sub_bcast(cols[j], i) for j in range(SUB) for i in range(j, SUB)}
        rows_m = [sub_bcast(mat[p], i) for i in range(SUB)]
        rows_x = [sub_bcast(aug[p], i) for i in range(SUB)]
        low, inv, root = {}, [], []
        for j in range(SUB):
            inv.append(1.0 / piv[j, j])
            root.append(lax.rsqrt(piv[j, j]))
            for i in range(j + 1, SUB):
                low[i, j] = piv[i, j] * inv[j]
            for i in range(j + 1, SUB):
                for k in range(j + 1, i + 1):
                    piv[i, k] = piv[i, k] - low[i, j] * piv[k, j]
                rows_m[i] = rows_m[i] - low[i, j] * rows_m[j]
                rows_x[i] = rows_x[i] - low[i, j] * rows_x[j]
        u_rows = rows_m[0] * root[0]
        w_rows = rows_x[0] * root[0]
        for i in range(1, SUB):
            u_rows = jnp.where(sub == i, rows_m[i] * root[i], u_rows)
            w_rows = jnp.where(sub == i, rows_x[i] * root[i], w_rows)
        put_u(p, u_rows)
        put_w(p, w_rows)
        if p + 1 == panels:
            break
        back_m = [rows_m[i] * inv[i] for i in range(SUB)]
        back_x = [rows_x[i] * inv[i] for i in range(SUB)]
        for i in range(SUB - 2, -1, -1):
            for j in range(SUB - 1, i, -1):
                back_m[i] = back_m[i] - low[j, i] * back_m[j]
                back_x[i] = back_x[i] - low[j, i] * back_x[j]
        for q in range(p + 1, panels):
            coef = [lane_bcast(mat[q], base + j) for j in range(SUB)]
            mat[q] = mat[q] - tree_sum([coef[j] * back_m[j] for j in range(SUB)])
            aug[q] = aug[q] - tree_sum([coef[j] * back_x[j] for j in range(SUB)])


def kernel(sizes, a_ref, out_ref, l_st, w_st, a_row, u_st, d_buf, u_buf, zero_buf,
           l_sem, w_sem, a_sem, out_sem, send_sem):
    row_size, col_size, rep_size = sizes
    rows_blk, cols_blk, blk, _ = a_ref.shape
    num = rows_blk * row_size
    chips = col_size * rep_size
    ring = chips * row_size
    slots = a_row.shape[0]
    twin = max(num - ring, 0)
    row, col, rep = lax.axis_index("row"), lax.axis_index("col"), lax.axis_index("rep")

    def snake(y, x):
        return jnp.where(y % 2 == 0, x, col_size - 1 - x)

    me = (rep * col_size + snake(rep, col)) * row_size + row

    def place(dev):
        chip = dev // row_size
        y = chip // col_size
        return {"rep": y, "col": snake(y, chip % col_size), "row": dev % row_size}

    def last_row(dev):
        return jnp.where(dev < twin, dev + ring, dev)

    def packed(big, small):
        return small * num - (small * (small - 1)) // 2 + big - small

    def send(src, dst, sem, where):
        pltpu.make_async_remote_copy(
            src_ref=src, dst_ref=dst, send_sem=send_sem, recv_sem=sem,
            device_id=where, device_id_type=MESH,
        ).start()

    def wait_block(ref, sem):
        pltpu.make_async_copy(ref, ref, sem).wait()

    barrier = pltpu.get_barrier_semaphore()

    @pl.loop(1, ring)
    def _(t):
        pl.semaphore_signal(barrier, inc=1, device_id=place((me + t) % ring), device_id_type=MESH)

    zero_buf[...] = jnp.zeros_like(zero_buf)
    u_st[...] = jnp.zeros_like(u_st)

    @pl.loop(0, rows_blk)
    def _(i):
        @pl.loop(0, cols_blk)
        def _(j):
            @pl.when(j * col_size + col > i * row_size + row)
            def _():
                pltpu.make_async_copy(zero_buf, out_ref.at[i, j], out_sem).start()

    pl.semaphore_wait(barrier, ring - 1)

    @pl.loop(0, cols_blk)
    def _(jj):
        for to_col in range(col_size):
            for s in range(slots):
                dest = (rep * col_size + snake(rep, to_col)) * row_size + row
                big = dest + s * ring
                j = jj * col_size + col

                @pl.when((big < num) & (j <= big))
                def _():
                    src, dst = a_ref.at[big // row_size, jj], a_row.at[s, j]

                    @pl.when(col == to_col)
                    def _():
                        pltpu.make_async_copy(src, dst, a_sem.at[s, j]).start()

                    @pl.when(col != to_col)
                    def _():
                        send(src, dst, a_sem.at[s, j], {"col": to_col})

    def to_later(src, dst, sem, big, lo, hi):
        @pl.loop(lo, hi)
        def _(t):
            dest = (me + t) % ring

            @pl.when(last_row(dest) > big)
            def _():
                send(src, dst, sem, place(dest))

    def to_output(idx, big, small):
        src, dst = l_st.at[idx], out_ref.at[big // row_size, small // col_size]
        to_col = small % col_size
        for to_rep in range(rep_size):
            here = (rep == to_rep) & (col == to_col)

            @pl.when(here)
            def _():
                pltpu.make_async_copy(src, dst, out_sem).start()

            @pl.when(jnp.logical_not(here))
            def _():
                send(src, dst, out_sem, {"rep": to_rep, "col": to_col})

    @pl.loop(-1, num - 1)
    def _(i):
        @pl.when((i >= 0) & (last_row(me) > i) & (i % ring != me))
        def _():
            wait_block(w_st.at[i], w_sem.at[i])

        @pl.loop(0, slots)
        def _(s):
            big = me + s * ring
            idx = packed(big, i)
            critical = big == i + 1
            follow = (big < num) & (big > i) & (i >= 0)

            @pl.when(follow)
            def _():
                wait_block(a_row.at[s, i], a_sem.at[s, i])
                gap = big - i
                half = pl.multiple_of((1 - gap % 2) * blk, blk)
                l_st[idx] = dot_nt(a_row[s, i] - u_st[s, gap // 2, :, pl.ds(half, blk)], w_st[i])
                to_later(l_st.at[idx], l_st.at[idx], l_sem.at[idx], big, 1, jnp.where(critical, 2, ring))

                @pl.when(jnp.logical_not(critical))
                def _():
                    to_output(idx, big, i)

                @pl.loop(jnp.maximum(i, jnp.where(s > 0, me, -1)) + 1, big)
                def _(j):
                    there = packed(j, i)
                    wait_block(l_st.at[there], l_sem.at[there])

                mine = l_st[idx]

                @pl.loop(0, (gap + 1) // 2)
                def _(g):
                    pair = l_st[pl.ds(idx - 2 * g - 1, 2)].reshape(2 * blk, blk)
                    u_st[s, g] = u_st[s, g] + dot_nt(mine, pair)

            @pl.when(critical & (big < num))
            def _():
                wait_block(a_row.at[s, big], a_sem.at[s, big])
                d_buf[...] = a_row[s, big] - u_st[s, 0, :, blk:2 * blk]

                def put_u(p, val):
                    u_buf[SUB * p:SUB * p + SUB, :] = val

                def put_w(p, val):
                    w_st[big, SUB * p:SUB * p + SUB, :] = val

                factor_block([d_buf[SUB * q:SUB * q + SUB, :] for q in range(blk // SUB)], put_u, put_w)
                to_later(w_st.at[big], w_st.at[big], w_sem.at[big], big, 1, ring)

                @pl.when(follow)
                def _():
                    to_later(l_st.at[idx], l_st.at[idx], l_sem.at[idx], big, 2, ring)
                    to_output(idx, big, i)

                lane = lax.broadcasted_iota(jnp.int32, (blk, blk), 1)
                sub = lax.broadcasted_iota(jnp.int32, (blk, blk), 0)
                diag = packed(big, big)
                l_st[diag] = jnp.where(lane <= sub, u_buf[...].T, 0.0)
                to_output(diag, big, big)

    total = 0
    for s in range(slots):
        big = me + s * ring
        targets = num - jnp.maximum(big + 1, twin) - jnp.where(last_row(me) > big, 1, 0)
        own = (big - col + col_size) // col_size
        sent = (big + 1) * targets + (big + 1) * rep_size - own
        total = total + jnp.where(big < num, sent, 0)
        for to_col in range(col_size):
            other = (rep * col_size + snake(rep, to_col)) * row_size + row + s * ring
            dealt = (other - col + col_size) // col_size
            total = total + jnp.where((other < num) & (to_col != col), dealt, 0)
    chunk = 16

    @pl.loop(0, total // chunk)
    def _(t):
        wait_block(l_st.at[0:chunk], send_sem)

    @pl.loop(0, total % chunk)
    def _(t):
        wait_block(l_st.at[0], send_sem)

    wait_block(out_ref, out_sem)


def solution(mesh):
    sizes = tuple(mesh.shape[axis] for axis in ("row", "col", "rep"))
    grid_spec = P(("b", "row"), "col")

    def local_factor(a_loc):
        rows_blk, cols_blk, blk, _ = a_loc.shape
        num = rows_blk * sizes[0]
        ring = sizes[0] * sizes[1] * sizes[2]
        slots = -(-num // ring)
        assert slots <= 2
        f32 = jnp.float32
        dma = pltpu.SemaphoreType.DMA
        tri = num * (num + 1) // 2
        return pl.pallas_call(
            functools.partial(kernel, sizes),
            out_shape=jax.ShapeDtypeStruct(a_loc.shape, f32),
            in_specs=[pl.BlockSpec(memory_space=pl.ANY)],
            out_specs=pl.BlockSpec(memory_space=pl.ANY),
            scratch_shapes=[
                pltpu.VMEM((tri, blk, blk), f32),
                pltpu.VMEM((num, blk, blk), f32),
                pltpu.VMEM((slots, num, blk, blk), f32),
                pltpu.VMEM((slots, (num + 1) // 2, blk, 2 * blk), f32),
                pltpu.VMEM((blk, blk), f32),
                pltpu.VMEM((blk, blk), f32),
                pltpu.VMEM((blk, blk), f32),
                dma((tri,)),
                dma((num,)),
                dma((slots, num)),
                dma,
                dma,
            ],
            compiler_params=pltpu.CompilerParams(
                collective_id=0, has_side_effects=True, vmem_limit_bytes=67043328,
            ),
        )(a_loc)

    return jax.shard_map(local_factor, mesh=mesh, in_specs=grid_spec, out_specs=grid_spec, check_vma=False)
```

time: 5270 us -> 763 us (0.14)
  waiting for transfers between devices: 3730 us -> 0 us
  other arithmetic: 989 us -> 0 us
  Pallas kernels: 0 us -> 752 us
  matrix products: 255 us -> 0 us
  local copies, waits for them, and re-layouts: 171 us -> 9.83 us
  blocking collectives: 58.7 us -> 0 us
    psum x107 -> x0, waiting for transfers between devices: 3400 us -> none  [the longest x36 1340 us: local_factor(): col_sum = lax.psum(work_mat[first_row:, first_col], 'rep')]
    another operation x181 -> x0, other arithmetic: 832 us -> none  [the longest x108 450 us: local_factor(): diag_fac = jnp.tril(jnp.linalg.cholesky(lax.psum(diag_mine, 'row')))]
    pallas_call x0 -> x1, Pallas kernels: none -> 752 us  [local_factor(): pl.pallas_call(functools.partial(kernel, sizes), out_shape=jax.ShapeDtype...]
    all_gather x22 -> x0, waiting for transfers between devices: 328 us -> none  [local_factor(): gathered = lax.all_gather(panel_row, 'row', axis=1)]
    dot_general x35 -> x0, matrix products: 188 us -> none  [local_factor(): jnp.einsum('tak,uck->tuac', row_share, col_share, precision=lax.Precision...]
    select_n x72 -> x0, other arithmetic: 104 us -> none  [the longest x36 52 us: local_factor(): diag_mine = jnp.where(row_idx == step_row, col_sum[0], 0.0)]
    another operation x36 -> x0, matrix products: 67.5 us -> none  [local_factor(): lax.linalg.triangular_solve(diag_fac, col_sum.reshape(tail_rows * blk_siz...]
    all_gather x13 -> x0, blocking collectives: 58.7 us -> none  [local_factor(): gathered = lax.all_gather(panel_row, 'row', axis=1)]
  transfers between devices with their start and end apart: 129 -> 0, of which waited for: 129 -> 0; matrix products, arithmetic and copies ran while one was open for 0% -> 0% of each run, Pallas kernels for 0% -> 0%
where the time goes in v1:
time: 763 us; the launch traced here: 762 us
  Pallas kernels  752 us (99%)
  local copies, waits for them, and re-layouts  9.83 us (1%)
    pallas_call x1, Pallas kernels, local_factor(): pl.pallas_call(functools.partial(kernel, sizes), out_shape=jax.ShapeDtype...  752 us

profile of v1, /device:TPU:103, one launch (start us, length us, event | category | flops | bytes accessed | tf_op | source)
XLA Modules:
  0.0 762.0 jit_solution(3786436410502238356)
XLA Ops:
  0.0 752.1 %shard_map.17 = f32[18,9,128,128]{3,2,1,0:T(8,128)} custom-call(f32[18,9,128,128]{3,2,1,0:T(8,128)} %a_ref.1), custom_call_target="tpu_custom_call" | custom-call | tf_op jit(solution)/shard_map/pallas_call | solution.py:276
  752.1 9.8 %copy.3 = f32[18,9,128,128]{3,2,1,0:T(8,128)} copy(f32[18,9,128,128]{3,2,1,0:T(8,128)} %shard_map.17) | data formatting | bytes 21233664

commit v2 on v1

--- a/solution.py
+++ b/solution.py
@@ -8,6 +8,8 @@
 from jax.sharding import PartitionSpec as P
 
 SUB = 8
+NEAR = 2
+UNROLL = 4
 MESH = pl.DeviceIdType.MESH
 
 
@@ -76,7 +78,7 @@
             aug[q] = aug[q] - tree_sum([coef[j] * back_x[j] for j in range(SUB)])
 
 
-def kernel(sizes, a_ref, out_ref, l_st, w_st, a_row, u_st, d_buf, u_buf, zero_buf,
+def kernel(sizes, a_ref, out_ref, l_st, w_st, a_row, d_acc, acc, u_buf, zero_buf, count,
            l_sem, w_sem, a_sem, out_sem, send_sem):
     row_size, col_size, rep_size = sizes
     rows_blk, cols_blk, blk, _ = a_ref.shape
@@ -90,20 +92,23 @@
     def snake(y, x):
         return jnp.where(y % 2 == 0, x, col_size - 1 - x)
 
-    me = (rep * col_size + snake(rep, col)) * row_size + row
-
-    def place(dev):
-        chip = dev // row_size
-        y = chip // col_size
-        return {"rep": y, "col": snake(y, chip % col_size), "row": dev % row_size}
+    chip = rep * col_size + snake(rep, col)
+    me = chip * row_size + row
+
+    def place(other_chip, other_row):
+        y = other_chip // col_size
+        return {"rep": y, "col": snake(y, other_chip % col_size), "row": other_row}
 
     def last_row(dev):
         return jnp.where(dev < twin, dev + ring, dev)
 
+    my_last = last_row(me)
+
     def packed(big, small):
-        return small * num - (small * (small - 1)) // 2 + big - small
+        return (big * (big + 1)) // 2 + small
 
     def send(src, dst, sem, where):
+        count[0] = count[0] + 1
         pltpu.make_async_remote_copy(
             src_ref=src, dst_ref=dst, send_sem=send_sem, recv_sem=sem,
             device_id=where, device_id_type=MESH,
@@ -116,10 +121,13 @@
 
     @pl.loop(1, ring)
     def _(t):
-        pl.semaphore_signal(barrier, inc=1, device_id=place((me + t) % ring), device_id_type=MESH)
-
+        dev = (me + t) % ring
+        pl.semaphore_signal(
+            barrier, inc=1, device_id=place(dev // row_size, dev % row_size), device_id_type=MESH)
+
+    count[0] = 0
     zero_buf[...] = jnp.zeros_like(zero_buf)
-    u_st[...] = jnp.zeros_like(u_st)
+    d_acc[...] = jnp.zeros_like(d_acc)
 
     @pl.loop(0, rows_blk)
     def _(i):
@@ -131,13 +139,11 @@
 
     pl.semaphore_wait(barrier, ring - 1)
 
-    @pl.loop(0, cols_blk)
-    def _(jj):
+    def deal(jj):
+        j = jj * col_size + col
         for to_col in range(col_size):
             for s in range(slots):
-                dest = (rep * col_size + snake(rep, to_col)) * row_size + row
-                big = dest + s * ring
-                j = jj * col_size + col
+                big = (rep * col_size + snake(rep, to_col)) * row_size + row + s * ring
 
                 @pl.when((big < num) & (j <= big))
                 def _():
@@ -151,34 +157,68 @@
                     def _():
                         send(src, dst, a_sem.at[s, j], {"col": to_col})
 
-    def to_later(src, dst, sem, big, lo, hi):
+    def to_partner(ref, sem, big):
+        for other in range(row_size):
+            @pl.when((row != other) & (last_row(chip * row_size + other) > big))
+            def _():
+                send(ref, ref, sem, {"row": other})
+
+    def to_chips(ref, sem, big, lo, hi, both):
         @pl.loop(lo, hi)
         def _(t):
-            dest = (me + t) % ring
-
-            @pl.when(last_row(dest) > big)
-            def _():
-                send(src, dst, sem, place(dest))
-
-    def to_output(idx, big, small):
+            dest = (chip + t) % chips
+            for shift in range(row_size):
+                core = (row + row_size - 1 - shift) % row_size
+                wanted = last_row(dest * row_size + core) > big
+                if shift < row_size - 1:
+                    wanted = wanted & (t <= both)
+
+                @pl.when(wanted)
+                def _():
+                    send(ref, ref, sem, place(dest, core))
+
+    def own_output(idx, big, small, everyone):
         src, dst = l_st.at[idx], out_ref.at[big // row_size, small // col_size]
         to_col = small % col_size
         for to_rep in range(rep_size):
-            here = (rep == to_rep) & (col == to_col)
+            dest = (to_rep * col_size + snake(jnp.int32(to_rep), to_col)) * row_size + row
+            here = dest == me
 
             @pl.when(here)
             def _():
                 pltpu.make_async_copy(src, dst, out_sem).start()
 
-            @pl.when(jnp.logical_not(here))
+            @pl.when(jnp.logical_not(here) & (everyone | (last_row(dest) <= big)))
             def _():
                 send(src, dst, out_sem, {"rep": to_rep, "col": to_col})
+
+    def held_output(idx, big, small):
+        @pl.when((big % row_size == row) & (small % col_size == col))
+        def _():
+            pltpu.make_async_copy(
+                l_st.at[idx], out_ref.at[big // row_size, small // col_size], out_sem).start()
+
+    deal(0)
 
     @pl.loop(-1, num - 1)
     def _(i):
-        @pl.when((i >= 0) & (last_row(me) > i) & (i % ring != me))
+        @pl.when((i >= 0) & (i + 1 < cols_blk))
         def _():
-            wait_block(w_st.at[i], w_sem.at[i])
+            deal(i + 1)
+
+        owner = i % ring
+        owner_chip = owner // row_size
+        waits = (i >= 0) & (my_last > i) & (owner != me)
+
+        @pl.when(waits)
+        def _():
+            early = (i % row_size == row) & (owner_chip != chip)
+
+            @pl.loop(jnp.where(early, jnp.maximum(i - NEAR, 0), 0), i)
+            def _(j):
+                idx = packed(i, j)
+                wait_block(l_st.at[idx], l_sem.at[idx])
+                held_output(idx, i, j)
 
         @pl.loop(0, slots)
         def _(s):
@@ -189,32 +229,47 @@
 
             @pl.when(follow)
             def _():
+                mine, theirs = packed(big, 0), packed(i, 0)
+                acc[...] = jnp.zeros_like(acc)
+
+                @pl.loop(0, i // UNROLL)
+                def _(g):
+                    base = g * UNROLL
+                    acc[...] += tree_sum(
+                        [dot_nt(l_st[mine + base + u], l_st[theirs + base + u]) for u in range(UNROLL)])
+
+                @pl.loop(i // UNROLL * UNROLL, i)
+                def _(j):
+                    acc[...] += dot_nt(l_st[mine + j], l_st[theirs + j])
+
                 wait_block(a_row.at[s, i], a_sem.at[s, i])
-                gap = big - i
-                half = pl.multiple_of((1 - gap % 2) * blk, blk)
-                l_st[idx] = dot_nt(a_row[s, i] - u_st[s, gap // 2, :, pl.ds(half, blk)], w_st[i])
-                to_later(l_st.at[idx], l_st.at[idx], l_sem.at[idx], big, 1, jnp.where(critical, 2, ring))
+                rest = a_row[s, i] - acc[...]
+
+                @pl.when(waits & ((s == 0) | (me <= i)))
+                def _():
+                    wait_block(w_st.at[i], w_sem.at[i])
+
+                    @pl.when((i % row_size == row) & (owner_chip != chip)
+                             & (owner_chip != (chip + chips - 1) % chips))
+                    def _():
+                        to_partner(w_st.at[i], w_sem.at[i], i)
+
+                l_new = dot_nt(rest, w_st[i])
+                l_st[idx] = l_new
+                both = jnp.where(big - i <= NEAR, chips, 0)
+                to_partner(l_st.at[idx], l_sem.at[idx], big)
+                to_chips(l_st.at[idx], l_sem.at[idx], big, 1, jnp.where(critical, 2, chips), both)
 
                 @pl.when(jnp.logical_not(critical))
                 def _():
-                    to_output(idx, big, i)
-
-                @pl.loop(jnp.maximum(i, jnp.where(s > 0, me, -1)) + 1, big)
-                def _(j):
-                    there = packed(j, i)
-                    wait_block(l_st.at[there], l_sem.at[there])
-
-                mine = l_st[idx]
-
-                @pl.loop(0, (gap + 1) // 2)
-                def _(g):
-                    pair = l_st[pl.ds(idx - 2 * g - 1, 2)].reshape(2 * blk, blk)
-                    u_st[s, g] = u_st[s, g] + dot_nt(mine, pair)
+                    own_output(idx, big, i, False)
+
+                d_acc[s] = d_acc[s] + dot_nt(l_new, l_new)
 
             @pl.when(critical & (big < num))
             def _():
                 wait_block(a_row.at[s, big], a_sem.at[s, big])
-                d_buf[...] = a_row[s, big] - u_st[s, 0, :, blk:2 * blk]
+                acc[...] = a_row[s, big] - d_acc[s]
 
                 def put_u(p, val):
                     u_buf[SUB * p:SUB * p + SUB, :] = val
@@ -222,38 +277,39 @@
                 def put_w(p, val):
                     w_st[big, SUB * p:SUB * p + SUB, :] = val
 
-                factor_block([d_buf[SUB * q:SUB * q + SUB, :] for q in range(blk // SUB)], put_u, put_w)
-                to_later(w_st.at[big], w_st.at[big], w_sem.at[big], big, 1, ring)
+                factor_block([acc[SUB * q:SUB * q + SUB, :] for q in range(blk // SUB)], put_u, put_w)
+                to_partner(w_st.at[big], w_sem.at[big], big)
+                to_chips(w_st.at[big], w_sem.at[big], big, 1, chips, 1)
 
                 @pl.when(follow)
                 def _():
-                    to_later(l_st.at[idx], l_st.at[idx], l_sem.at[idx], big, 2, ring)
-                    to_output(idx, big, i)
+                    to_chips(l_st.at[idx], l_sem.at[idx], big, 2, chips, chips)
+                    own_output(idx, big, i, False)
 
                 lane = lax.broadcasted_iota(jnp.int32, (blk, blk), 1)
                 sub = lax.broadcasted_iota(jnp.int32, (blk, blk), 0)
                 diag = packed(big, big)
                 l_st[diag] = jnp.where(lane <= sub, u_buf[...].T, 0.0)
-                to_output(diag, big, big)
-
-    total = 0
-    for s in range(slots):
-        big = me + s * ring
-        targets = num - jnp.maximum(big + 1, twin) - jnp.where(last_row(me) > big, 1, 0)
-        own = (big - col + col_size) // col_size
-        sent = (big + 1) * targets + (big + 1) * rep_size - own
-        total = total + jnp.where(big < num, sent, 0)
-        for to_col in range(col_size):
-            other = (rep * col_size + snake(rep, to_col)) * row_size + row + s * ring
-            dealt = (other - col + col_size) // col_size
-            total = total + jnp.where((other < num) & (to_col != col), dealt, 0)
+                own_output(diag, big, big, True)
+
+        @pl.when(i >= NEAR)
+        def _():
+            @pl.loop(i + 1, my_last)
+            def _(j):
+                @pl.when((j % row_size == row) & (j % ring != me))
+                def _():
+                    idx = packed(j, i - NEAR)
+                    wait_block(l_st.at[idx], l_sem.at[idx])
+                    to_partner(l_st.at[idx], l_sem.at[idx], j)
+                    held_output(idx, j, i - NEAR)
+
     chunk = 16
 
-    @pl.loop(0, total // chunk)
+    @pl.loop(0, count[0] // chunk)
     def _(t):
         wait_block(l_st.at[0:chunk], send_sem)
 
-    @pl.loop(0, total % chunk)
+    @pl.loop(0, count[0] % chunk)
     def _(t):
         wait_block(l_st.at[0], send_sem)
 
@@ -282,10 +338,11 @@
                 pltpu.VMEM((tri, blk, blk), f32),
                 pltpu.VMEM((num, blk, blk), f32),
                 pltpu.VMEM((slots, num, blk, blk), f32),
-                pltpu.VMEM((slots, (num + 1) // 2, blk, 2 * blk), f32),
+                pltpu.VMEM((slots, blk, blk), f32),
                 pltpu.VMEM((blk, blk), f32),
                 pltpu.VMEM((blk, blk), f32),
                 pltpu.VMEM((blk, blk), f32),
+                pltpu.SMEM((1,), jnp.int32),
                 dma((tri,)),
                 dma((num,)),
                 dma((slots, num)),

time: 763 us -> 497 us (0.65)
  Pallas kernels: 752 us -> 487 us
    pallas_call x1, Pallas kernels: 752 us -> 487 us  [local_factor(): pl.pallas_call(functools.partial(kernel, sizes), out_shape=jax.ShapeDtype...]
where the time goes in v2:
time: 497 us; the launch traced here: 496 us
  Pallas kernels  487 us (98%)
  local copies, waits for them, and re-layouts  9.83 us (2%)
    pallas_call x1, Pallas kernels, local_factor(): pl.pallas_call(functools.partial(kernel, sizes), out_shape=jax.ShapeDtype...  487 us

profile of v2, /device:TPU:103, one launch (start us, length us, event | category | flops | bytes accessed | tf_op | source)
XLA Modules:
  0.0 496.4 jit_solution(11566643746225099500)
XLA Ops:
  0.0 486.6 %shard_map.17 = f32[18,9,128,128]{3,2,1,0:T(8,128)} custom-call(f32[18,9,128,128]{3,2,1,0:T(8,128)} %a_ref.1), custom_call_target="tpu_custom_call" | custom-call | tf_op jit(solution)/shard_map/pallas_call | solution.py:332
  486.6 9.8 %copy.3 = f32[18,9,128,128]{3,2,1,0:T(8,128)} copy(f32[18,9,128,128]{3,2,1,0:T(8,128)} %shard_map.17) | data formatting | bytes 21233664

commit v3 on v2

--- a/solution.py
+++ b/solution.py
@@ -9,6 +9,7 @@
 
 SUB = 8
 NEAR = 2
+LAG = 3
 UNROLL = 4
 MESH = pl.DeviceIdType.MESH
 
@@ -100,9 +101,19 @@
         return {"rep": y, "col": snake(y, other_chip % col_size), "row": other_row}
 
     def last_row(dev):
-        return jnp.where(dev < twin, dev + ring, dev)
+        return jnp.where(dev >= ring - twin, dev + twin, dev)
+
+    def chip_at(y, x):
+        return y * col_size + snake(y, x)
+
+    def chip_last(other_chip):
+        return last_row(other_chip * row_size + row_size - 1)
+
+    def owner_of(big):
+        return jnp.where(big >= ring, big - twin, big)
 
     my_last = last_row(me)
+    x_first = row == 0
 
     def packed(big, small):
         return (big * (big + 1)) // 2 + small
@@ -143,9 +154,13 @@
         j = jj * col_size + col
         for to_col in range(col_size):
             for s in range(slots):
-                big = (rep * col_size + snake(rep, to_col)) * row_size + row + s * ring
-
-                @pl.when((big < num) & (j <= big))
+                dev = chip_at(rep, to_col) * row_size + row
+                big = dev + s * twin
+                real = j <= big
+                if s:
+                    real = real & (dev >= ring - twin)
+
+                @pl.when(real)
                 def _():
                     src, dst = a_ref.at[big // row_size, jj], a_row.at[s, j]
 
@@ -177,20 +192,60 @@
                 def _():
                     send(ref, ref, sem, place(dest, core))
 
-    def own_output(idx, big, small, everyone):
+    def to_col_peers(ref, sem, big, whole):
+        for shift in range(1, col_size):
+            x = (col + shift) % col_size
+            wanted = chip_last(chip_at(jnp.where(whole, rep_size - 1, rep), x)) > big
+
+            @pl.when(wanted)
+            def _():
+                send(ref, ref, sem, {"col": x})
+
+    def to_rep_peers(ref, sem, big, whole):
+        for shift in range(1, rep_size):
+            y = (rep + shift) % rep_size
+            wanted = jnp.where(whole, chip_last(y * col_size + col_size - 1), chip_last(chip_at(y, col))) > big
+
+            @pl.when(wanted)
+            def _():
+                send(ref, ref, sem, {"rep": y})
+
+    def arrived(idx, big, small):
+        to_partner(l_st.at[idx], l_sem.at[idx], big)
+
+        @pl.when(my_last > big)
+        def _():
+            held_output(idx, big, small)
+
+    def passed_down(small):
+        return small < num - 1 - LAG - rep_size
+
+    def reaches(big, small, x):
+        there = chip_at(rep, x)
+        relays = x_first & (big - small > NEAR) & (chip_last(chip_at(rep_size - 1, x)) > big)
+        return (last_row(there * row_size + row) > big) | relays
+
+    def own_output(idx, big, small, diagonal):
         src, dst = l_st.at[idx], out_ref.at[big // row_size, small // col_size]
         to_col = small % col_size
-        for to_rep in range(rep_size):
-            dest = (to_rep * col_size + snake(jnp.int32(to_rep), to_col)) * row_size + row
-            here = dest == me
-
-            @pl.when(here)
-            def _():
-                pltpu.make_async_copy(src, dst, out_sem).start()
-
-            @pl.when(jnp.logical_not(here) & (everyone | (last_row(dest) <= big)))
-            def _():
-                send(src, dst, out_sem, {"rep": to_rep, "col": to_col})
+        down = passed_down(small) & (big != small)
+
+        @pl.when(to_col == col)
+        def _():
+            pltpu.make_async_copy(src, dst, out_sem).start()
+
+        @pl.when(down & (to_col != col) & jnp.logical_not(reaches(big, small, to_col)))
+        def _():
+            send(src, src, l_sem.at[idx], {"col": to_col})
+
+        @pl.when(jnp.logical_not(down))
+        def _():
+            for to_rep in range(rep_size):
+                dest = chip_at(jnp.int32(to_rep), to_col) * row_size + row
+
+                @pl.when((dest != me) & (diagonal | (last_row(dest) <= big)))
+                def _():
+                    send(src, dst, out_sem, {"rep": to_rep, "col": to_col})
 
     def held_output(idx, big, small):
         @pl.when((big % row_size == row) & (small % col_size == col))
@@ -206,7 +261,7 @@
         def _():
             deal(i + 1)
 
-        owner = i % ring
+        owner = owner_of(i)
         owner_chip = owner // row_size
         waits = (i >= 0) & (my_last > i) & (owner != me)
 
@@ -218,14 +273,20 @@
             def _(j):
                 idx = packed(i, j)
                 wait_block(l_st.at[idx], l_sem.at[idx])
+
+                @pl.when(early & (owner_chip != (chip + chips - 1) % chips))
+                def _():
+                    to_partner(l_st.at[idx], l_sem.at[idx], i)
+
                 held_output(idx, i, j)
 
         @pl.loop(0, slots)
         def _(s):
-            big = me + s * ring
+            big = me + s * twin
             idx = packed(big, i)
-            critical = big == i + 1
-            follow = (big < num) & (big > i) & (i >= 0)
+            real = (s == 0) | (me >= ring - twin)
+            critical = real & (big == i + 1)
+            follow = real & (big > i) & (i >= 0)
 
             @pl.when(follow)
             def _():
@@ -235,8 +296,9 @@
                 @pl.loop(0, i // UNROLL)
                 def _(g):
                     base = g * UNROLL
-                    acc[...] += tree_sum(
-                        [dot_nt(l_st[mine + base + u], l_st[theirs + base + u]) for u in range(UNROLL)])
+                    acc[...] += dot_nt(
+                        jnp.concatenate([l_st[mine + base + u] for u in range(UNROLL)], axis=1),
+                        jnp.concatenate([l_st[theirs + base + u] for u in range(UNROLL)], axis=1))
 
                 @pl.loop(i // UNROLL * UNROLL, i)
                 def _(j):
@@ -256,9 +318,18 @@
 
                 l_new = dot_nt(rest, w_st[i])
                 l_st[idx] = l_new
-                both = jnp.where(big - i <= NEAR, chips, 0)
-                to_partner(l_st.at[idx], l_sem.at[idx], big)
-                to_chips(l_st.at[idx], l_sem.at[idx], big, 1, jnp.where(critical, 2, chips), both)
+                new, new_sem = l_st.at[idx], l_sem.at[idx]
+                near = big - i <= NEAR
+                to_partner(new, new_sem, big)
+
+                @pl.when(near)
+                def _():
+                    to_chips(new, new_sem, big, 1, jnp.where(critical, 2, chips), 1)
+
+                @pl.when(jnp.logical_not(near))
+                def _():
+                    to_col_peers(new, new_sem, big, x_first)
+                    to_rep_peers(new, new_sem, big, jnp.logical_not(x_first))
 
                 @pl.when(jnp.logical_not(critical))
                 def _():
@@ -266,7 +337,7 @@
 
                 d_acc[s] = d_acc[s] + dot_nt(l_new, l_new)
 
-            @pl.when(critical & (big < num))
+            @pl.when(critical)
             def _():
                 wait_block(a_row.at[s, big], a_sem.at[s, big])
                 acc[...] = a_row[s, big] - d_acc[s]
@@ -283,7 +354,7 @@
 
                 @pl.when(follow)
                 def _():
-                    to_chips(l_st.at[idx], l_sem.at[idx], big, 2, chips, chips)
+                    to_chips(l_st.at[idx], l_sem.at[idx], big, 2, chips, 1)
                     own_output(idx, big, i, False)
 
                 lane = lax.broadcasted_iota(jnp.int32, (blk, blk), 1)
@@ -292,16 +363,84 @@
                 l_st[diag] = jnp.where(lane <= sub, u_buf[...].T, 0.0)
                 own_output(diag, big, big, True)
 
+        def relay(source, along):
+            for s in range(slots):
+                big = source + s * twin
+                real = big - i >= NEAR
+                if s:
+                    real = real & (source >= ring - twin)
+                if along == "rep":
+                    real = real & (chip_last(chip_at(rep_size - 1, col)) > big)
+                else:
+                    real = real & (chip_last(rep * col_size + col_size - 1) > big)
+
+                @pl.when(real)
+                def _():
+                    idx = packed(big, i - 1)
+                    wait_block(l_st.at[idx], l_sem.at[idx])
+                    if along == "rep":
+                        to_rep_peers(l_st.at[idx], l_sem.at[idx], big, False)
+                    else:
+                        to_col_peers(l_st.at[idx], l_sem.at[idx], big, False)
+                    arrived(idx, big, i - 1)
+
+        @pl.when((i >= 1) & x_first)
+        def _():
+            for shift in range(1, col_size):
+                relay(chip_at(rep, (col + shift) % col_size) * row_size + row, "rep")
+
+        @pl.when((i >= 1) & jnp.logical_not(x_first))
+        def _():
+            for shift in range(1, rep_size):
+                relay(chip_at((rep + shift) % rep_size, col) * row_size + row, "col")
+
         @pl.when(i >= NEAR)
         def _():
             @pl.loop(i + 1, my_last)
             def _(j):
-                @pl.when((j % row_size == row) & (j % ring != me))
+                source = owner_of(j) // row_size
+                y = source // col_size
+                second = jnp.where(x_first, y != rep, snake(y, source % col_size) != col)
+
+                @pl.when((j % row_size == row) & second)
                 def _():
                     idx = packed(j, i - NEAR)
                     wait_block(l_st.at[idx], l_sem.at[idx])
-                    to_partner(l_st.at[idx], l_sem.at[idx], j)
-                    held_output(idx, j, i - NEAR)
+                    arrived(idx, j, i - NEAR)
+
+        @pl.loop(0, rep_size)
+        def _(gap):
+            small = i - LAG - gap
+            y = rep + gap
+
+            @pl.when((small >= 0) & (small % col_size == col) & (y < rep_size) & passed_down(small))
+            def _():
+                @pl.loop(0, col_size)
+                def _(x):
+                    dev = chip_at(y, x) * row_size + row
+
+                    for s in range(slots):
+                        big = dev + s * twin
+                        real = big > small
+                        if s:
+                            real = real & (dev >= ring - twin)
+
+                        @pl.when(real)
+                        def _():
+                            idx = packed(big, small)
+                            held = (gap == 0) & ((dev == me) | (my_last > big))
+
+                            @pl.when(jnp.where(gap == 0, (dev != me) & jnp.logical_not(reaches(big, small, col)), True))
+                            def _():
+                                wait_block(l_st.at[idx], l_sem.at[idx])
+
+                            @pl.when(jnp.logical_not(held))
+                            def _():
+                                held_output(idx, big, small)
+
+                            @pl.when(rep > 0)
+                            def _():
+                                send(l_st.at[idx], l_st.at[idx], l_sem.at[idx], {"rep": rep - 1})
 
     chunk = 16
 

time: 497 us -> 389 us (0.78)
  Pallas kernels: 487 us -> 379 us
    pallas_call x1, Pallas kernels: 487 us -> 379 us  [local_factor(): pl.pallas_call(functools.partial(kernel, sizes), out_shape=jax.ShapeDtype...]
where the time goes in v3:
time: 389 us; the launch traced here: 388 us
  Pallas kernels  379 us (97%)
  local copies, waits for them, and re-layouts  9.83 us (3%)
    pallas_call x1, Pallas kernels, local_factor(): pl.pallas_call(functools.partial(kernel, sizes), out_shape=jax.ShapeDtype...  379 us
    unnamed x1, local copies, waits for them, and re-layouts  9.83 us

profile of v3, /device:TPU:103, one launch (start us, length us, event | category | flops | bytes accessed | tf_op | source)
XLA Modules:
  0.0 388.4 jit_solution(10395285399436632585)
XLA Ops:
  0.0 378.5 %shard_map.17 = f32[18,9,128,128]{3,2,1,0:T(8,128)} custom-call(f32[18,9,128,128]{3,2,1,0:T(8,128)} %a_ref.1), custom_call_target="tpu_custom_call" | custom-call | tf_op jit(solution)/shard_map/pallas_call | solution.py:471
  378.6 9.8 %copy.3 = f32[18,9,128,128]{3,2,1,0:T(8,128)} copy(f32[18,9,128,128]{3,2,1,0:T(8,128)} %shard_map.17) | data formatting | bytes 21233664

commit v4 on v3

--- a/solution.py
+++ b/solution.py
@@ -79,6 +79,14 @@
             aug[q] = aug[q] - tree_sum([coef[j] * back_x[j] for j in range(SUB)])
 
 
+def div(num, den):
+    return lax.div(num, jnp.int32(den))
+
+
+def rem(num, den):
+    return lax.rem(num, jnp.int32(den))
+
+
 def kernel(sizes, a_ref, out_ref, l_st, w_st, a_row, d_acc, acc, u_buf, zero_buf, count,
            l_sem, w_sem, a_sem, out_sem, send_sem):
     row_size, col_size, rep_size = sizes
@@ -91,14 +99,14 @@
     row, col, rep = lax.axis_index("row"), lax.axis_index("col"), lax.axis_index("rep")
 
     def snake(y, x):
-        return jnp.where(y % 2 == 0, x, col_size - 1 - x)
+        return jnp.where(rem(y, 2) == 0, x, col_size - 1 - x)
 
     chip = rep * col_size + snake(rep, col)
     me = chip * row_size + row
 
     def place(other_chip, other_row):
-        y = other_chip // col_size
-        return {"rep": y, "col": snake(y, other_chip % col_size), "row": other_row}
+        y = div(other_chip, col_size)
+        return {"rep": y, "col": snake(y, other_chip - y * col_size), "row": other_row}
 
     def last_row(dev):
         return jnp.where(dev >= ring - twin, dev + twin, dev)
@@ -116,7 +124,7 @@
     x_first = row == 0
 
     def packed(big, small):
-        return (big * (big + 1)) // 2 + small
+        return div(big * (big + 1), 2) + small
 
     def send(src, dst, sem, where):
         count[0] = count[0] + 1
@@ -132,9 +140,9 @@
 
     @pl.loop(1, ring)
     def _(t):
-        dev = (me + t) % ring
+        dev = rem(me + t, ring)
         pl.semaphore_signal(
-            barrier, inc=1, device_id=place(dev // row_size, dev % row_size), device_id_type=MESH)
+            barrier, inc=1, device_id=place(div(dev, row_size), rem(dev, row_size)), device_id_type=MESH)
 
     count[0] = 0
     zero_buf[...] = jnp.zeros_like(zero_buf)
@@ -162,7 +170,7 @@
 
                 @pl.when(real)
                 def _():
-                    src, dst = a_ref.at[big // row_size, jj], a_row.at[s, j]
+                    src, dst = a_ref.at[div(big, row_size), jj], a_row.at[s, j]
 
                     @pl.when(col == to_col)
                     def _():
@@ -181,9 +189,9 @@
     def to_chips(ref, sem, big, lo, hi, both):
         @pl.loop(lo, hi)
         def _(t):
-            dest = (chip + t) % chips
+            dest = rem(chip + t, chips)
             for shift in range(row_size):
-                core = (row + row_size - 1 - shift) % row_size
+                core = rem(row + row_size - 1 - shift, row_size)
                 wanted = last_row(dest * row_size + core) > big
                 if shift < row_size - 1:
                     wanted = wanted & (t <= both)
@@ -194,7 +202,7 @@
 
     def to_col_peers(ref, sem, big, whole):
         for shift in range(1, col_size):
-            x = (col + shift) % col_size
+            x = rem(col + shift, col_size)
             wanted = chip_last(chip_at(jnp.where(whole, rep_size - 1, rep), x)) > big
 
             @pl.when(wanted)
@@ -203,7 +211,7 @@
 
     def to_rep_peers(ref, sem, big, whole):
         for shift in range(1, rep_size):
-            y = (rep + shift) % rep_size
+            y = rem(rep + shift, rep_size)
             wanted = jnp.where(whole, chip_last(y * col_size + col_size - 1), chip_last(chip_at(y, col))) > big
 
             @pl.when(wanted)
@@ -226,8 +234,8 @@
         return (last_row(there * row_size + row) > big) | relays
 
     def own_output(idx, big, small, diagonal):
-        src, dst = l_st.at[idx], out_ref.at[big // row_size, small // col_size]
-        to_col = small % col_size
+        src, dst = l_st.at[idx], out_ref.at[div(big, row_size), div(small, col_size)]
+        to_col = rem(small, col_size)
         down = passed_down(small) & (big != small)
 
         @pl.when(to_col == col)
@@ -248,37 +256,48 @@
                     send(src, dst, out_sem, {"rep": to_rep, "col": to_col})
 
     def held_output(idx, big, small):
-        @pl.when((big % row_size == row) & (small % col_size == col))
+        @pl.when((rem(big, row_size) == row) & (rem(small, col_size) == col))
         def _():
             pltpu.make_async_copy(
-                l_st.at[idx], out_ref.at[big // row_size, small // col_size], out_sem).start()
+                l_st.at[idx], out_ref.at[div(big, row_size), div(small, col_size)], out_sem).start()
 
     deal(0)
+    deal(1)
 
     @pl.loop(-1, num - 1)
     def _(i):
-        @pl.when((i >= 0) & (i + 1 < cols_blk))
-        def _():
-            deal(i + 1)
+        @pl.when((i >= 0) & (rem(i, col_size) == 0) & (div(i, col_size) + 2 < cols_blk))
+        def _():
+            deal(div(i, col_size) + 2)
 
         owner = owner_of(i)
-        owner_chip = owner // row_size
+        owner_chip = div(owner, row_size)
+        before = owner_chip == rem(chip + chips - 1, chips)
+        same_core = rem(i, row_size) == row
         waits = (i >= 0) & (my_last > i) & (owner != me)
 
-        @pl.when(waits)
-        def _():
-            early = (i % row_size == row) & (owner_chip != chip)
-
-            @pl.loop(jnp.where(early, jnp.maximum(i - NEAR, 0), 0), i)
+        far = jnp.maximum(i - NEAR, 0)
+        theirs = packed(i, 0)
+
+        @pl.when(waits & jnp.logical_not(same_core & (owner_chip != chip)))
+        def _():
+            @pl.loop(0, far)
             def _(j):
-                idx = packed(i, j)
+                wait_block(l_st.at[theirs + j], l_sem.at[theirs + j])
+
+        def wait_near():
+            @pl.loop(far, i)
+            def _(j):
+                idx = theirs + j
                 wait_block(l_st.at[idx], l_sem.at[idx])
 
-                @pl.when(early & (owner_chip != (chip + chips - 1) % chips))
-                def _():
-                    to_partner(l_st.at[idx], l_sem.at[idx], i)
-
-                held_output(idx, i, j)
+                @pl.when(same_core & (owner_chip != chip))
+                def _():
+                    @pl.when(jnp.logical_not(before))
+                    def _():
+                        to_partner(l_st.at[idx], l_sem.at[idx], i)
+
+                    held_output(idx, i, j)
 
         @pl.loop(0, slots)
         def _(s):
@@ -290,29 +309,38 @@
 
             @pl.when(follow)
             def _():
-                mine, theirs = packed(big, 0), packed(i, 0)
+                mine = packed(big, 0)
+                first_slot = (s == 0) | (me <= i)
                 acc[...] = jnp.zeros_like(acc)
-
-                @pl.loop(0, i // UNROLL)
+                quads = div(far, UNROLL)
+
+                @pl.loop(0, quads)
                 def _(g):
                     base = g * UNROLL
                     acc[...] += dot_nt(
                         jnp.concatenate([l_st[mine + base + u] for u in range(UNROLL)], axis=1),
                         jnp.concatenate([l_st[theirs + base + u] for u in range(UNROLL)], axis=1))
 
-                @pl.loop(i // UNROLL * UNROLL, i)
-                def _(j):
-                    acc[...] += dot_nt(l_st[mine + j], l_st[theirs + j])
+                @pl.when(waits & first_slot)
+                def _():
+                    wait_near()
+
+                @pl.loop(quads, div(i + UNROLL - 1, UNROLL))
+                def _(g):
+                    base = g * UNROLL
+                    last = [jnp.minimum(base + u, i - 1) for u in range(UNROLL)]
+                    acc[...] += dot_nt(
+                        jnp.concatenate([jnp.where(base + u < i, l_st[mine + last[u]], 0.0) for u in range(UNROLL)], axis=1),
+                        jnp.concatenate([l_st[theirs + last[u]] for u in range(UNROLL)], axis=1))
 
                 wait_block(a_row.at[s, i], a_sem.at[s, i])
                 rest = a_row[s, i] - acc[...]
 
-                @pl.when(waits & ((s == 0) | (me <= i)))
+                @pl.when(waits & first_slot)
                 def _():
                     wait_block(w_st.at[i], w_sem.at[i])
 
-                    @pl.when((i % row_size == row) & (owner_chip != chip)
-                             & (owner_chip != (chip + chips - 1) % chips))
+                    @pl.when(same_core & (owner_chip != chip) & jnp.logical_not(before))
                     def _():
                         to_partner(w_st.at[i], w_sem.at[i], i)
 
@@ -363,92 +391,100 @@
                 l_st[diag] = jnp.where(lane <= sub, u_buf[...].T, 0.0)
                 own_output(diag, big, big, True)
 
-        def relay(source, along):
-            for s in range(slots):
-                big = source + s * twin
-                real = big - i >= NEAR
-                if s:
-                    real = real & (source >= ring - twin)
-                if along == "rep":
-                    real = real & (chip_last(chip_at(rep_size - 1, col)) > big)
-                else:
-                    real = real & (chip_last(rep * col_size + col_size - 1) > big)
-
-                @pl.when(real)
-                def _():
-                    idx = packed(big, i - 1)
-                    wait_block(l_st.at[idx], l_sem.at[idx])
+        soon = (me == i + 2) | ((me >= ring - twin) & (me + twin == i + 2))
+        now = (me == i + 1) | ((me >= ring - twin) & (me + twin == i + 1))
+
+        @pl.loop(jnp.where(now, jnp.maximum(i - 1, -1), i), jnp.where(soon, i, i + 1))
+        def _(q):
+            def relay(source, along):
+                for s in range(slots):
+                    big = source + s * twin
+                    real = big - q >= NEAR
+                    if s:
+                        real = real & (source >= ring - twin)
                     if along == "rep":
-                        to_rep_peers(l_st.at[idx], l_sem.at[idx], big, False)
+                        real = real & (chip_last(chip_at(rep_size - 1, col)) > big)
                     else:
-                        to_col_peers(l_st.at[idx], l_sem.at[idx], big, False)
-                    arrived(idx, big, i - 1)
-
-        @pl.when((i >= 1) & x_first)
-        def _():
-            for shift in range(1, col_size):
-                relay(chip_at(rep, (col + shift) % col_size) * row_size + row, "rep")
-
-        @pl.when((i >= 1) & jnp.logical_not(x_first))
-        def _():
-            for shift in range(1, rep_size):
-                relay(chip_at((rep + shift) % rep_size, col) * row_size + row, "col")
-
-        @pl.when(i >= NEAR)
-        def _():
-            @pl.loop(i + 1, my_last)
-            def _(j):
-                source = owner_of(j) // row_size
-                y = source // col_size
-                second = jnp.where(x_first, y != rep, snake(y, source % col_size) != col)
-
-                @pl.when((j % row_size == row) & second)
-                def _():
-                    idx = packed(j, i - NEAR)
-                    wait_block(l_st.at[idx], l_sem.at[idx])
-                    arrived(idx, j, i - NEAR)
-
-        @pl.loop(0, rep_size)
-        def _(gap):
-            small = i - LAG - gap
-            y = rep + gap
-
-            @pl.when((small >= 0) & (small % col_size == col) & (y < rep_size) & passed_down(small))
-            def _():
-                @pl.loop(0, col_size)
-                def _(x):
-                    dev = chip_at(y, x) * row_size + row
-
-                    for s in range(slots):
-                        big = dev + s * twin
-                        real = big > small
-                        if s:
-                            real = real & (dev >= ring - twin)
-
-                        @pl.when(real)
-                        def _():
-                            idx = packed(big, small)
-                            held = (gap == 0) & ((dev == me) | (my_last > big))
-
-                            @pl.when(jnp.where(gap == 0, (dev != me) & jnp.logical_not(reaches(big, small, col)), True))
+                        real = real & (chip_last(rep * col_size + col_size - 1) > big)
+
+                    @pl.when(real)
+                    def _():
+                        idx = packed(big, q - 1)
+                        wait_block(l_st.at[idx], l_sem.at[idx])
+                        if along == "rep":
+                            to_rep_peers(l_st.at[idx], l_sem.at[idx], big, False)
+                        else:
+                            to_col_peers(l_st.at[idx], l_sem.at[idx], big, False)
+                        arrived(idx, big, q - 1)
+
+            @pl.when((q >= 1) & x_first)
+            def _():
+                for shift in range(1, col_size):
+                    relay(chip_at(rep, rem(col + shift, col_size)) * row_size + row, "rep")
+
+            @pl.when((q >= 1) & jnp.logical_not(x_first))
+            def _():
+                for shift in range(1, rep_size):
+                    relay(chip_at(rem(rep + shift, rep_size), col) * row_size + row, "col")
+
+            @pl.when(q >= NEAR)
+            def _():
+                first = q + 1 + rem(q + 1 + row, row_size)
+
+                @pl.loop(0, div(jnp.maximum(my_last - first, 0) + row_size - 1, row_size))
+                def _(t):
+                    j = first + t * row_size
+                    source = div(owner_of(j), row_size)
+                    y = div(source, col_size)
+                    second = jnp.where(x_first, y != rep, snake(y, source - y * col_size) != col)
+
+                    @pl.when(second)
+                    def _():
+                        idx = packed(j, q - NEAR)
+                        wait_block(l_st.at[idx], l_sem.at[idx])
+                        arrived(idx, j, q - NEAR)
+
+            @pl.loop(0, rep_size)
+            def _(gap):
+                small = q - LAG - gap
+                y = rep + gap
+
+                @pl.when((small >= 0) & (rem(jnp.maximum(small, 0), col_size) == col) & (y < rep_size) & passed_down(small))
+                def _():
+                    @pl.loop(0, col_size)
+                    def _(x):
+                        dev = chip_at(y, x) * row_size + row
+
+                        for s in range(slots):
+                            big = dev + s * twin
+                            real = big > small
+                            if s:
+                                real = real & (dev >= ring - twin)
+
+                            @pl.when(real)
                             def _():
-                                wait_block(l_st.at[idx], l_sem.at[idx])
-
-                            @pl.when(jnp.logical_not(held))
-                            def _():
-                                held_output(idx, big, small)
-
-                            @pl.when(rep > 0)
-                            def _():
-                                send(l_st.at[idx], l_st.at[idx], l_sem.at[idx], {"rep": rep - 1})
+                                idx = packed(big, small)
+                                held = (gap == 0) & ((dev == me) | (my_last > big))
+
+                                @pl.when(jnp.where(gap == 0, (dev != me) & jnp.logical_not(reaches(big, small, col)), True))
+                                def _():
+                                    wait_block(l_st.at[idx], l_sem.at[idx])
+
+                                @pl.when(jnp.logical_not(held))
+                                def _():
+                                    held_output(idx, big, small)
+
+                                @pl.when(rep > 0)
+                                def _():
+                                    send(l_st.at[idx], l_st.at[idx], l_sem.at[idx], {"rep": rep - 1})
 
     chunk = 16
 
-    @pl.loop(0, count[0] // chunk)
+    @pl.loop(0, div(count[0], chunk))
     def _(t):
         wait_block(l_st.at[0:chunk], send_sem)
 
-    @pl.loop(0, count[0] % chunk)
+    @pl.loop(0, rem(count[0], chunk))
     def _(t):
         wait_block(l_st.at[0], send_sem)
 

time: 389 us -> 359 us (0.923)
  Pallas kernels: 379 us -> 349 us
    pallas_call x1, Pallas kernels: 379 us -> 349 us  [local_factor(): pl.pallas_call(functools.partial(kernel, sizes), out_shape=jax.ShapeDtype...]
where the time goes in v4:
time: 359 us; the launch traced here: 358 us
  Pallas kernels  349 us (97%)
  local copies, waits for them, and re-layouts  9.83 us (3%)
    pallas_call x1, Pallas kernels, local_factor(): pl.pallas_call(functools.partial(kernel, sizes), out_shape=jax.ShapeDtype...  349 us
    unnamed x1, local copies, waits for them, and re-layouts  9.83 us

profile of v4, /device:TPU:103, one launch (start us, length us, event | category | flops | bytes accessed | tf_op | source)
XLA Modules:
  0.0 358.4 jit_solution(7047309976741840611)
XLA Ops:
  0.0 348.5 %shard_map.17 = f32[18,9,128,128]{3,2,1,0:T(8,128)} custom-call(f32[18,9,128,128]{3,2,1,0:T(8,128)} %a_ref.1), custom_call_target="tpu_custom_call" | custom-call | tf_op jit(solution)/shard_map/pallas_call | solution.py:507
  348.5 9.8 %copy.3 = f32[18,9,128,128]{3,2,1,0:T(8,128)} copy(f32[18,9,128,128]{3,2,1,0:T(8,128)} %shard_map.17) | data formatting | bytes 21233664

commit v5 on v4

--- a/solution.py
+++ b/solution.py
@@ -121,7 +121,11 @@
         return jnp.where(big >= ring, big - twin, big)
 
     my_last = last_row(me)
-    x_first = row == 0
+
+    def goes_x_first(y):
+        return (row == 0) | (y == rep_size - 2)
+
+    x_first = goes_x_first(rep)
 
     def packed(big, small):
         return div(big * (big + 1), 2) + small
@@ -148,15 +152,16 @@
     zero_buf[...] = jnp.zeros_like(zero_buf)
     d_acc[...] = jnp.zeros_like(d_acc)
 
-    @pl.loop(0, rows_blk)
-    def _(i):
-        @pl.loop(0, cols_blk)
-        def _(j):
-            @pl.when(j * col_size + col > i * row_size + row)
-            def _():
+    pl.semaphore_wait(barrier, ring - 1)
+
+    def clear_above():
+        @pl.loop(0, rows_blk)
+        def _(i):
+            first = div(i * row_size + row - col + col_size, col_size)
+
+            @pl.loop(jnp.maximum(first, 0), cols_blk)
+            def _(j):
                 pltpu.make_async_copy(zero_buf, out_ref.at[i, j], out_sem).start()
-
-    pl.semaphore_wait(barrier, ring - 1)
 
     def deal(jj):
         j = jj * col_size + col
@@ -264,6 +269,11 @@
     deal(0)
     deal(1)
 
+    @pl.when(me >= ring // 2)
+    def _():
+        clear_above()
+
+
     @pl.loop(-1, num - 1)
     def _(i):
         @pl.when((i >= 0) & (rem(i, col_size) == 0) & (div(i, col_size) + 2 < cols_blk))
@@ -390,6 +400,10 @@
                 diag = packed(big, big)
                 l_st[diag] = jnp.where(lane <= sub, u_buf[...].T, 0.0)
                 own_output(diag, big, big, True)
+
+                @pl.when((s == 0) & (me < ring // 2))
+                def _():
+                    clear_above()
 
         soon = (me == i + 2) | ((me >= ring - twin) & (me + twin == i + 2))
         now = (me == i + 1) | ((me >= ring - twin) & (me + twin == i + 1))
@@ -422,10 +436,12 @@
                 for shift in range(1, col_size):
                     relay(chip_at(rep, rem(col + shift, col_size)) * row_size + row, "rep")
 
-            @pl.when((q >= 1) & jnp.logical_not(x_first))
-            def _():
-                for shift in range(1, rep_size):
-                    relay(chip_at(rem(rep + shift, rep_size), col) * row_size + row, "col")
+            for shift in range(1, rep_size):
+                other = rem(rep + shift, rep_size)
+
+                @pl.when((q >= 1) & jnp.logical_not(goes_x_first(other)))
+                def _():
+                    relay(chip_at(other, col) * row_size + row, "col")
 
             @pl.when(q >= NEAR)
             def _():
@@ -436,7 +452,7 @@
                     j = first + t * row_size
                     source = div(owner_of(j), row_size)
                     y = div(source, col_size)
-                    second = jnp.where(x_first, y != rep, snake(y, source - y * col_size) != col)
+                    second = jnp.where(goes_x_first(y), y != rep, snake(y, source - y * col_size) != col)
 
                     @pl.when(second)
                     def _():

time: 359 us -> 357 us (level)
  no operation moved by 1% of the time
where the time goes in v5:
time: 357 us; the launch traced here: 356 us
  Pallas kernels  347 us (97%)
  local copies, waits for them, and re-layouts  9.83 us (3%)
    pallas_call x1, Pallas kernels, local_factor(): pl.pallas_call(functools.partial(kernel, sizes), out_shape=jax.ShapeDtype...  347 us
    unnamed x1, local copies, waits for them, and re-layouts  9.83 us

profile of v5, /device:TPU:103, one launch (start us, length us, event | category | flops | bytes accessed | tf_op | source)
XLA Modules:
  0.0 356.4 jit_solution(14861460354499642564)
XLA Ops:
  0.0 346.6 %shard_map.17 = f32[18,9,128,128]{3,2,1,0:T(8,128)} custom-call(f32[18,9,128,128]{3,2,1,0:T(8,128)} %a_ref.1), custom_call_target="tpu_custom_call" | custom-call | tf_op jit(solution)/shard_map/pallas_call | solution.py:523
  346.6 9.8 %copy.3 = f32[18,9,128,128]{3,2,1,0:T(8,128)} copy(f32[18,9,128,128]{3,2,1,0:T(8,128)} %shard_map.17) | data formatting | bytes 21233664
